TPU v7x, 32 devices: a whole 2x2x4 slice. The times are simulated.
32 devices in a mesh: groups: 2 (over y), expert: 4 (over x, core), tensor: 4 (over z).
Axes of the slice: x: 2, y: 2, z: 4, core: 2. Of those that a mesh axis runs over, the one named last changes fastest.
Arguments:
- tokens: bfloat16 [512, 4096], P(('groups', 'expert'), 'tensor'), parts along dimension 0, may hold values from -400 to 400
- norm_gain: float32 [4096], replicated, may hold values from 0.5 to 1.5
- w_gate: bfloat16 [4096, 65536], P(None, ('expert', 'tensor')), may hold values from -0.09375 to 0.09375
- w_up: bfloat16 [4096, 65536], P(None, ('expert', 'tensor')), may hold values from -0.09375 to 0.09375
- w_down: bfloat16 [65536, 4096], P(('expert', 'tensor')), may hold values from -0.0625 to 0.0625
- expert_ids: int32 [512, 2], P(('groups', 'expert')), parts along dimension 0, may hold values from 0 to 7, all different within a row; in each aligned block of 64 rows (0 to 63, 64 to 127, ...) at most 32 rows name the same one
- gate_weights: float32 [512, 2], P(('groups', 'expert')), parts along dimension 0, may hold values from 0.1 to 1
Outputs:
- moe_out: bfloat16 [512, 4096], P(('groups', 'expert'), 'tensor'), parts along dimension 0
There are 2 independent parts, one for each index of `groups`. A program takes and returns all parts, laid end to end along the dimension named above; an argument that names none is the same for every part. Nothing has to cross between parts.
Inputs may be any that keep to these rules, and one draw needn't show every extreme that they name: `expert_ids`: each request names two different experts. Within the rows of one device (aligned blocks of 64 rows) no expert is named by more than 32 rows, and in some blocks one expert is named by exactly 32 rows.
All inputs are finite; a program needn't handle non-finite values.
Results may differ from a plain program's by a relative error of at most 0.008.
Values may be sent and summed in bfloat16 or wider, within the bound.
A program may use at most 192 MiB of HBM per device.

v0:
```python
import jax
import jax.numpy as jnp
from jax import lax
from jax.sharding import PartitionSpec as P

EXPERTS = 8


def lookup(targets, token_table, valid_table):
    select = (targets[..., None] == jnp.arange(token_table.shape[0], dtype=jnp.int32)).astype(
        jnp.int32
    )
    token_at = jnp.sum(select[..., None] * token_table, axis=-2)
    valid_at = jnp.sum(select[..., None] * valid_table, axis=-2)
    return (token_at, valid_at)


def pack_rows(normed, targets, token_table, valid_table):
    token_at, valid_at = lookup(targets, token_table, valid_table)
    picked = jnp.take(normed, token_at.reshape(-1), axis=0)
    picked = picked.reshape(token_at.shape + (normed.shape[1],))
    return picked * valid_at[..., None].astype(jnp.bfloat16)


def per_device(tokens, norm_gain, w_gate, w_up, w_down, expert_ids, gate_weights):
    n_expert = lax.axis_size("expert")
    n_tensor = lax.axis_size("tensor")
    tok_rows = tokens.shape[0]
    width_local = tokens.shape[1]
    width_full = width_local * n_tensor
    capacity = tok_rows // 2
    per_expert = n_expert * n_tensor // EXPERTS
    tensor_index = lax.axis_index("tensor")
    peers = jnp.arange(n_expert, dtype=jnp.int32)
    own_targets = ((peers * n_tensor + tensor_index) // per_expert)[:, None]
    flat_ids = expert_ids.reshape(-1)
    onehot = (flat_ids[:, None] == jnp.arange(EXPERTS, dtype=jnp.int32)[None, :]).astype(jnp.int32)
    running = jnp.cumsum(onehot, axis=0)
    slot_of = jnp.sum(running * onehot, axis=1) - 1
    pair_token = jnp.arange(flat_ids.shape[0], dtype=jnp.int32) // 2
    slot_hits = onehot[:, :, None] * (
        slot_of[:, None, None] == jnp.arange(capacity, dtype=jnp.int32)[None, None, :]
    ).astype(jnp.int32)
    token_table = jnp.sum(slot_hits * pair_token[:, None, None], axis=0)
    valid_table = jnp.sum(slot_hits, axis=0)
    full_rows = lax.all_gather(tokens, "tensor", axis=1, tiled=True)
    values = full_rows.astype(jnp.float32)
    sum_squares = jnp.sum(values * values, axis=1)
    scale = lax.rsqrt(sum_squares / width_full + 1e-05)
    normed = (values * scale[:, None] * norm_gain[None, :]).astype(jnp.bfloat16)
    outbound = pack_rows(normed, own_targets, token_table, valid_table)
    own_block = lax.all_to_all(outbound, "expert", split_axis=0, concat_axis=0, tiled=True)
    items = own_block.shape[2]
    flattened = own_block.reshape(-1, own_block.shape[3])
    gate_act = jnp.dot(flattened, w_gate, preferred_element_type=jnp.float32)
    up_act = jnp.dot(flattened, w_up, preferred_element_type=jnp.float32)
    hidden = (jax.nn.silu(gate_act) * up_act).astype(jnp.bfloat16)
    partial_value = jnp.dot(hidden, w_down, preferred_element_type=jnp.float32)
    partial_value = partial_value.reshape(n_expert, 1, items, partial_value.shape[1])
    returned = lax.all_to_all(partial_value, "expert", split_axis=0, concat_axis=0, tiled=True)
    mixing = (
        jnp.arange(EXPERTS, dtype=jnp.int32)[:, None] == own_targets.reshape(-1)[None, :]
    ).astype(jnp.float32)
    out_width = returned.shape[3]
    by_expert = jnp.dot(
        mixing,
        returned.reshape(own_targets.size, -1),
        precision=lax.Precision.HIGHEST,
        preferred_element_type=jnp.float32,
    )
    by_expert = by_expert.reshape(EXPERTS * capacity, out_width)
    picks = jnp.take(by_expert, flat_ids * capacity + slot_of, axis=0)
    mixed = jnp.sum(picks.reshape(tok_rows, 2, out_width) * gate_weights[:, :, None], axis=1)
    mixed = lax.psum_scatter(mixed, "tensor", scatter_dimension=1, tiled=True)
    return mixed.astype(jnp.bfloat16)


def solution(mesh):
    in_specs = (
        P(("groups", "expert"), "tensor"),
        P(),
        P(None, ("expert", "tensor")),
        P(None, ("expert", "tensor")),
        P(("expert", "tensor"), None),
        P(("groups", "expert"), None),
        P(("groups", "expert"), None),
    )
    out_specs = P(("groups", "expert"), "tensor")
    return jax.shard_map(
        per_device, mesh=mesh, in_specs=in_specs, out_specs=out_specs, check_vma=False
    )
```

profile of v0, /device:TPU:0, one launch (start us, length us, event | category | flops | bytes accessed | tf_op | source)
XLA Modules:
  0.0 173.0 jit_solution(17244527256869342859)
XLA Ops:
  6.5 0.8 copy.25
  7.3 0.1 reshape.291
  7.4 0.1 fusion.12
  7.6 0.2 reduce_window_sum.11
  7.8 0.2 select_reduce_fusion
  8.0 0.1 fusion.16
  8.1 0.3 multiply_reduce_fusion.1
  8.4 0.1 multiply_reduce_fusion.2
  8.5 0.1 reshape.292
  8.6 17.6 %all_gather.3 = bf16[64,4096]{1,0:T(8,128)(2,1)S(1)} all-gather(bf16[64,1024]{1,0:T(8,128)(2,1)} %param.7), channel_id=1, replica_groups=mesh['groups'=2,'expert'=4,'tensor'=4] {'tensor'}, dimensions={1}, use_global_device_ids=true | all-gather | bytes 655360 | tf_op jit(solution)/shard_map/all_gather | solution.py:46
  26.2 0.2 fusion.7
  26.4 0.9 fusion.9
  27.4 1.2 gather_fusion
  28.6 0.2 select_multiply_fusion
  28.8 17.0 %all_to_all.10 = bf16[4,1,32,4096]{3,2,1,0:T(8,128)(2,1)S(1)} all-to-all(bf16[4,1,32,4096]{3,2,1,0:T(8,128)(2,1)S(1)} %select_multiply_fusion), channel_id=1, replica_groups=mesh['groups'=2,'expert'=4,'tensor'=4] {'expert'}, dimensions={0} | all-to-all | bytes 2097152 | tf_op jit(solution)/shard_map/all_to_all | solution.py:52
  45.7 12.9 %fusion.20 = f32[128,4096]{1,0:T(8,128)S(1)} fusion(bf16[128,4096]{1,0:T(8,128)(2,1)S(1)} %bitcast.26, bf16[4096,4096]{1,0:T(8,128)(2,1)} %param.9), kind=kOutput, calls=%fused_computation.56 | convolution fusion | flops 4294967296 | bytes 36700160 | tf_op jit(solution)/shard_map/dot_general | solution.py:55
  58.7 25.3 %fusion.1 = f32[128,4096]{1,0:T(8,128)} fusion(bf16[4096,4096]{1,0:T(8,128)(2,1)} %param.11, bf16[128,4096]{1,0:T(8,128)(2,1)S(1)} %bitcast.27, bf16[4096,4096]{1,0:T(8,128)(2,1)} %param.10, f32[128,4096]{1,0:T(8,128)S(1)} %fusion.20), kind=kOutput, calls=%fused_computation.4 | convolution fusion | flops 8593080320 | bytes 72351744 | tf_op jit(solution)/shard_map/dot_general | solution.py:58
  84.0 0.0 copy-start
  84.0 0.0 copy-start.1
  84.0 3.7 %all-to-all-start.1 = ((f32[4,1,32,4096]{3,2,1,0:T(8,128)}), f32[4,1,32,4096]{3,2,1,0:T(8,128)S(1)}, u32[]{:S(2)}, u32[]{:S(2)}) async-start(f32[4,1,32,4096]{3,2,1,0:T(8,128)} %bitcast.29), calls=%async_computation.1 | async-start | bytes 4194304 | tf_op jit(solution)/shard_map/all_to_all | solution.py:60
  87.8 0.2 reduce-scatter.2.cloned.1.call-start
  88.0 0.1 sub.19
  88.1 0.0 copy-done
  88.1 0.1 copy.31
  88.2 0.1 mul.167
  88.4 0.1 copy.26
  88.5 0.1 copy.27
  88.6 0.0 copy-done.1
  88.6 0.1 copy.32
  88.7 24.7 %all-to-all-done.1 = f32[4,1,32,4096]{3,2,1,0:T(8,128)S(1)} async-done(((f32[4,1,32,4096]{3,2,1,0:T(8,128)}), f32[4,1,32,4096]{3,2,1,0:T(8,128)S(1)}, u32[]{:S(2)}, u32[]{:S(2)}) %all-to-all-start.1) | async-done | bytes 2097184 | tf_op jit(solution)/shard_map/all_to_all | solution.py:60
  113.4 1.4 copy.33
  114.7 4.0 %fusion.14 = f32[8,131072]{1,0:T(8,128)} fusion(f32[4,131072]{1,0:T(4,128)S(1)} %bitcast.24, s32[4]{0:T(128)S(1)} %and_select_fusion.1), kind=kOutput, calls=%fused_computation.32 | convolution fusion | flops 50331680 | bytes 6291472 | tf_op jit(solution)/shard_map/dot_general | solution.py:65
  118.8 4.9 %reshape.296 = f32[256,4096]{1,0:T(8,128)} reshape(f32[8,131072]{1,0:T(8,128)} %fusion.14) | data formatting | bytes 8388608 | tf_op jit(solution)/shard_map/reshape | solution.py:71
  123.6 5.6 %gather_fusion.1 = f32[128,4096]{1,0:T(8,128)} fusion(f32[256,4096]{1,0:T(8,128)} %reshape.296, s32[1024]{0:T(1024)S(1)} %pad_clamp_fusion), kind=kCustom, calls=%fused_computation.1 | custom fusion | bytes 4194816 | tf_op jit(solution)/shard_map/jit(_take)/gather | solution.py:72
  129.3 2.5 %gather.15 = f32[64,2,4096]{2,1,0:T(2,128)S(1)} reshape(f32[128,4096]{1,0:T(8,128)} %gather_fusion.1) | data formatting | bytes 4194304 | tf_op jit(solution)/shard_map/jit(_take)/gather | solution.py:72
  131.8 4.5 %multiply_reduce_fusion = f32[64,4096]{1,0:T(8,128)} fusion(f32[64,2,4096]{2,1,0:T(2,128)S(1)} %gather.15, pred[64,2]{1,0:T(8,128)(4,1)S(1)} %copy.27, f32[64,2]{1,0:T(8,128)S(1)} %copy.32), kind=kLoop, calls=%fused_computation.5 | loop fusion | flops 1310720 | bytes 3146368 | tf_op jit(solution)/shard_map/reduce_sum | solution.py:73
  136.2 0.0 reduce-scatter.2.cloned.1.call-update
  136.3 28.3 %reduce-scatter.2.cloned.1.call-done = f32[64,1024]{1,0:T(8,128)} async-done(((f32[64,4096]{1,0:T(8,128)}), f32[64,1024]{1,0:T(8,128)}) %reduce-scatter.2.cloned.1.call-update) | async-done | bytes 262160 | tf_op jit(solution)/shard_map/reduce_scatter | solution.py:74
  164.6 1.6 convert_element_type.52
  (14 shorter events, 0.1 us)
Async XLA Ops:
  84.0 4.1 %copy-start = (s32[64,2]{0,1:T(2,128)S(1)}, s32[64,2]{0,1:T(2,128)}, u32[]{:S(2)}) copy-start(s32[64,2]{0,1:T(2,128)} %param.12) | copy-start | bytes 1540
  84.0 4.6 %copy-start.1 = (f32[64,2]{0,1:T(2,128)S(1)}, f32[64,2]{0,1:T(2,128)}, u32[]{:S(2)}) copy-start(f32[64,2]{0,1:T(2,128)} %param.13) | copy-start | bytes 1540
  84.0 29.4 %all-to-all-start.1 = ((f32[4,1,32,4096]{3,2,1,0:T(8,128)}), f32[4,1,32,4096]{3,2,1,0:T(8,128)S(1)}, u32[]{:S(2)}, u32[]{:S(2)}) async-start(f32[4,1,32,4096]{3,2,1,0:T(8,128)} %bitcast.29), calls=%async_computation.1 | async-start | bytes 4194304 | tf_op jit(solution)/shard_map/all_to_all | solution.py:60
  87.8 76.8 %reduce-scatter.2.cloned.1.call-start = ((), (), s32[]{:S(2)}) async-start(), calls=%async_computation.3 | async-start | bytes 1310720 | tf_op jit(solution)/shard_map/reduce_scatter | solution.py:74
Sparse Core Ops, SparseCore 0:
  136.4 28.1 reduce-scatter.1
where the time goes:
time: 173 us
  waiting for transfers between devices  53 us (31%)
  matrix products  42.3 us (24%)
  blocking collectives  34.6 us (20%)
  local copies, waits for them, and re-layouts  17.2 us (10%)
  between operations  13.6 us (8%)
  other arithmetic  8.46 us (5%)
  starting transfers between devices  3.96 us (2%)
    reduce_scatter x1, waiting for transfers between devices, per_device(): mixed = lax.psum_scatter(mixed, 'tensor', scatter_dimension=1, tiled=True)  28.3 us
    dot_general x1, matrix products, per_device(): partial_value = jnp.dot(hidden, w_down, preferred_element_type=jnp.float32)  25.3 us
    all_to_all x1, waiting for transfers between devices, per_device(): lax.all_to_all(partial_value, 'expert', split_axis=0, concat_axis=0, tile...  24.7 us
    all_gather x1, blocking collectives, per_device(): full_rows = lax.all_gather(tokens, 'tensor', axis=1, tiled=True)  17.6 us
    all_to_all x1, blocking collectives, per_device(): lax.all_to_all(outbound, 'expert', split_axis=0, concat_axis=0, tiled=True)  17 us
    dot_general x1, matrix products, per_device(): gate_act = jnp.dot(flattened, w_gate, preferred_element_type=jnp.float32)  12.9 us
    gather x2, local copies, waits for them, and re-layouts, per_device(): picks = jnp.take(by_expert, flat_ids * capacity + slot_of, axis=0)  8.11 us
    reshape x1, local copies, waits for them, and re-layouts, per_device(): by_expert = by_expert.reshape(EXPERTS * capacity, out_width)  4.86 us
  transfers between devices with their start and end apart: 2, of which 2 were waited for; matrix products, arithmetic and copies ran while one was open for 0% of the time, Pallas kernels for 0%

commit v1 on v0

--- a/solution.py
+++ b/solution.py
@@ -43,7 +43,14 @@
     ).astype(jnp.int32)
     token_table = jnp.sum(slot_hits * pair_token[:, None, None], axis=0)
     valid_table = jnp.sum(slot_hits, axis=0)
-    full_rows = lax.all_gather(tokens, "tensor", axis=1, tiled=True)
+    ring = [tokens]
+    for hop in range(3):
+        ring.append(lax.ppermute(ring[-1], "tensor", [(dev, (dev + 1) % 4) for dev in range(4)]))
+    full_rows = jnp.roll(
+        jnp.concatenate(ring[::-1], axis=1),
+        (lax.axis_index("tensor") + 1) * ring[0].shape[1],
+        axis=1,
+    )
     values = full_rows.astype(jnp.float32)
     sum_squares = jnp.sum(values * values, axis=1)
     scale = lax.rsqrt(sum_squares / width_full + 1e-05)

time: 173 us -> 173 us (level)
  blocking collectives: 34.6 us -> 17 us
  waiting for transfers between devices: 53 us -> 66 us
  starting transfers between devices: 3.96 us -> 7.02 us
    all_gather x1 -> x0, blocking collectives: 17.6 us -> none  [per_device(): full_rows = lax.all_gather(tokens, 'tensor', axis=1, tiled=True)]
    ppermute x0 -> x3, waiting for transfers between devices: none -> 16.3 us  [per_device(): lax.ppermute(ring[-1], 'tensor', [(dev, (dev + 1) % 4) for dev in range(4)])]
    reduce_scatter x1, waiting for transfers between devices: 28.3 us -> 24.7 us  [per_device(): mixed = lax.psum_scatter(mixed, 'tensor', scatter_dimension=1, tiled=True)]
    ppermute x0 -> x3, starting transfers between devices: none -> 3.06 us  [per_device(): lax.ppermute(ring[-1], 'tensor', [(dev, (dev + 1) % 4) for dev in range(4)])]
  transfers between devices with their start and end apart: 2 -> 5, of which waited for: 2 -> 5; matrix products, arithmetic and copies ran while one was open for 0% -> 2% of each run, Pallas kernels for 0% -> 0%
where the time goes in v1:
time: 173 us
  waiting for transfers between devices  66 us (38%)
  matrix products  42.3 us (24%)
  local copies, waits for them, and re-layouts  18.2 us (11%)
  blocking collectives  17 us (10%)
  between operations  13.6 us (8%)
  other arithmetic  8.43 us (5%)
  starting transfers between devices  7.02 us (4%)
    dot_general x1, matrix products, per_device(): partial_value = jnp.dot(hidden, w_down, preferred_element_type=jnp.float32)  25.3 us
    all_to_all x1, waiting for transfers between devices, per_device(): lax.all_to_all(partial_value, 'expert', split_axis=0, concat_axis=0, tile...  24.9 us
    reduce_scatter x1, waiting for transfers between devices, per_device(): mixed = lax.psum_scatter(mixed, 'tensor', scatter_dimension=1, tiled=True)  24.7 us
    all_to_all x1, blocking collectives, per_device(): lax.all_to_all(outbound, 'expert', split_axis=0, concat_axis=0, tiled=True)  17 us
    ppermute x3, waiting for transfers between devices, per_device(): lax.ppermute(ring[-1], 'tensor', [(dev, (dev + 1) % 4) for dev in range(4)])  16.3 us
    dot_general x1, matrix products, per_device(): gate_act = jnp.dot(flattened, w_gate, preferred_element_type=jnp.float32)  12.9 us
    gather x2, local copies, waits for them, and re-layouts, per_device(): picks = jnp.take(by_expert, flat_ids * capacity + slot_of, axis=0)  8.11 us
    reshape x1, local copies, waits for them, and re-layouts, per_device(): by_expert = by_expert.reshape(EXPERTS * capacity, out_width)  4.86 us
  transfers between devices with their start and end apart: 5, of which 5 were waited for; matrix products, arithmetic and copies ran while one was open for 2% of the time, Pallas kernels for 0%

profile of v1, /device:TPU:0, one launch (start us, length us, event | category | flops | bytes accessed | tf_op | source)
XLA Modules:
  0.0 172.5 jit_solution(6577529786523449463)
XLA Ops:
  6.5 0.0 copy-start
  6.5 0.0 copy-start.1
  6.5 3.1 %collective-permute-start = (bf16[64,1024]{1,0:T(8,128)(2,1)}, bf16[64,1024]{1,0:T(8,128)(2,1)S(1)}, u32[]{:S(2)}, u32[]{:S(2)}) collective-permute-start(bf16[64,1024]{1,0:T(8,128)(2,1)} %param.7), channel_id=1, source_target_pairs={{0,1},{1,2},{2,3},{3,0},{4,5},{5,6},{6,7},{7,4},{8,9},{9,10},{10,1... | collective-permute-start | bytes 393224 | tf_op jit(solution)/shard_map/ppermute | solution.py:48
  9.6 0.8 copy.25
  10.4 0.7 broadcast_multiply_fusion
  11.0 0.1 reshape.291
  11.2 0.1 fusion.12
  11.3 0.2 reduce_window_sum.11
  11.5 0.2 select_reduce_fusion
  11.7 0.1 fusion.16
  11.8 0.3 multiply_reduce_fusion.1
  12.2 0.1 multiply_reduce_fusion.2
  12.2 0.1 reshape.292
  12.3 0.1 copy.31
  12.4 0.1 mul.171
  12.6 2.8 %collective-permute-done = bf16[64,1024]{1,0:T(8,128)(2,1)S(1)} collective-permute-done((bf16[64,1024]{1,0:T(8,128)(2,1)}, bf16[64,1024]{1,0:T(8,128)(2,1)S(1)}, u32[]{:S(2)}, u32[]{:S(2)}) %collective-permute-start) | collective-permute-done | bytes 131104 | tf_op jit(solution)/shard_map/ppermute | solution.py:48
  15.4 0.0 collective-permute-start.1
  15.4 6.8 %collective-permute-done.1 = bf16[64,1024]{1,0:T(8,128)(2,1)S(1)} collective-permute-done((bf16[64,1024]{1,0:T(8,128)(2,1)S(1)}, bf16[64,1024]{1,0:T(8,128)(2,1)S(1)}, u32[]{:S(2)}, u32[]{:S(2)}) %collective-permute-start.1) | collective-permute-done | bytes 131104 | tf_op jit(solution)/shard_map/ppermute | solution.py:48
  22.2 0.0 collective-permute-start.2
  22.2 6.7 %collective-permute-done.2 = bf16[64,1024]{1,0:T(8,128)(2,1)S(1)} collective-permute-done((bf16[64,1024]{1,0:T(8,128)(2,1)S(1)}, bf16[64,1024]{1,0:T(8,128)(2,1)S(1)}, u32[]{:S(2)}, u32[]{:S(2)}) %collective-permute-start.2) | collective-permute-done | bytes 131104 | tf_op jit(solution)/shard_map/ppermute | solution.py:48
  29.0 0.9 constant_dynamic-update-slice_fusion.4
  29.9 0.0 copy-done
  30.0 0.2 fusion.7
  30.2 0.0 copy-done.1
  30.2 0.2 fusion.9
  30.4 1.2 gather_fusion
  31.6 0.2 select_multiply_fusion
  31.8 17.0 %all_to_all.10 = bf16[4,1,32,4096]{3,2,1,0:T(8,128)(2,1)S(1)} all-to-all(bf16[4,1,32,4096]{3,2,1,0:T(8,128)(2,1)S(1)} %select_multiply_fusion), channel_id=1, replica_groups=mesh['groups'=2,'expert'=4,'tensor'=4] {'expert'}, dimensions={0} | all-to-all | bytes 2097152 | tf_op jit(solution)/shard_map/all_to_all | solution.py:59
  48.8 12.9 %fusion.20 = f32[128,4096]{1,0:T(8,128)S(1)} fusion(bf16[128,4096]{1,0:T(8,128)(2,1)S(1)} %bitcast.26, bf16[4096,4096]{1,0:T(8,128)(2,1)} %param.9), kind=kOutput, calls=%fused_computation.64 | convolution fusion | flops 4294967296 | bytes 36700160 | tf_op jit(solution)/shard_map/dot_general | solution.py:62
  61.7 25.3 %fusion.1 = f32[128,4096]{1,0:T(8,128)} fusion(bf16[4096,4096]{1,0:T(8,128)(2,1)} %param.11, bf16[128,4096]{1,0:T(8,128)(2,1)S(1)} %bitcast.27, bf16[4096,4096]{1,0:T(8,128)(2,1)} %param.10, f32[128,4096]{1,0:T(8,128)S(1)} %fusion.20), kind=kOutput, calls=%fused_computation.4 | convolution fusion | flops 8593080320 | bytes 72351744 | tf_op jit(solution)/shard_map/dot_general | solution.py:65
  87.1 3.7 %all-to-all-start.1 = ((f32[4,1,32,4096]{3,2,1,0:T(8,128)}), f32[4,1,32,4096]{3,2,1,0:T(8,128)S(1)}, u32[]{:S(2)}, u32[]{:S(2)}) async-start(f32[4,1,32,4096]{3,2,1,0:T(8,128)} %bitcast.29), calls=%async_computation.1 | async-start | bytes 4194304 | tf_op jit(solution)/shard_map/all_to_all | solution.py:67
  90.8 0.2 reduce-scatter.2.cloned.1.call-start
  91.0 0.1 sub.23
  91.2 0.1 copy.26
  91.2 0.0 copy-done.2
  91.3 0.1 copy.27
  91.4 0.0 copy-done.3
  91.4 0.1 copy.32
  91.5 24.9 %all-to-all-done.1 = f32[4,1,32,4096]{3,2,1,0:T(8,128)S(1)} async-done(((f32[4,1,32,4096]{3,2,1,0:T(8,128)}), f32[4,1,32,4096]{3,2,1,0:T(8,128)S(1)}, u32[]{:S(2)}, u32[]{:S(2)}) %all-to-all-start.1) | async-done | bytes 2097184 | tf_op jit(solution)/shard_map/all_to_all | solution.py:67
  116.4 1.4 copy.33
  117.8 4.0 %fusion.14 = f32[8,131072]{1,0:T(8,128)} fusion(f32[4,131072]{1,0:T(4,128)S(1)} %bitcast.24, s32[4]{0:T(128)S(1)} %and_select_fusion.1), kind=kOutput, calls=%fused_computation.40 | convolution fusion | flops 50331680 | bytes 6291472 | tf_op jit(solution)/shard_map/dot_general | solution.py:72
  121.8 4.9 %reshape.296 = f32[256,4096]{1,0:T(8,128)} reshape(f32[8,131072]{1,0:T(8,128)} %fusion.14) | data formatting | bytes 8388608 | tf_op jit(solution)/shard_map/reshape | solution.py:78
  126.7 5.6 %gather_fusion.1 = f32[128,4096]{1,0:T(8,128)} fusion(f32[256,4096]{1,0:T(8,128)} %reshape.296, s32[1024]{0:T(1024)S(1)} %get-tuple-element.9), kind=kCustom, calls=%fused_computation.1 | custom fusion | bytes 4194816 | tf_op jit(solution)/shard_map/jit(_take)/gather | solution.py:79
  132.3 2.5 %gather.15 = f32[64,2,4096]{2,1,0:T(2,128)S(1)} reshape(f32[128,4096]{1,0:T(8,128)} %gather_fusion.1) | data formatting | bytes 4194304 | tf_op jit(solution)/shard_map/jit(_take)/gather | solution.py:79
  134.8 4.5 %multiply_reduce_fusion = f32[64,4096]{1,0:T(8,128)} fusion(f32[64,2,4096]{2,1,0:T(2,128)S(1)} %gather.15, pred[64,2]{1,0:T(8,128)(4,1)S(1)} %copy.27, f32[64,2]{1,0:T(8,128)S(1)} %copy.32), kind=kLoop, calls=%fused_computation.5 | loop fusion | flops 1310720 | bytes 3146368 | tf_op jit(solution)/shard_map/reduce_sum | solution.py:80
  139.3 0.0 reduce-scatter.2.cloned.1.call-update
  139.3 24.7 %reduce-scatter.2.cloned.1.call-done = f32[64,1024]{1,0:T(8,128)} async-done(((f32[64,4096]{1,0:T(8,128)}), f32[64,1024]{1,0:T(8,128)}) %reduce-scatter.2.cloned.1.call-update) | async-done | bytes 262160 | tf_op jit(solution)/shard_map/reduce_scatter | solution.py:81
  164.0 1.6 convert_element_type.52
  (21 shorter events, 0.2 us)
Async XLA Ops:
  6.5 23.4 %copy-start = (bf16[64,1024]{1,0:T(8,128)(2,1)S(1)}, bf16[64,1024]{1,0:T(8,128)(2,1)}, u32[]{:S(2)}) copy-start(bf16[64,1024]{1,0:T(8,128)(2,1)} %param.7) | copy-start | bytes 393220
  6.5 23.7 %copy-start.1 = (f32[4096]{0:T(1024)S(1)}, f32[4096]{0:T(1024)}, u32[]{:S(2)}) copy-start(f32[4096]{0:T(1024)} %param.8) | copy-start | bytes 49156
  6.5 8.9 %collective-permute-start = (bf16[64,1024]{1,0:T(8,128)(2,1)}, bf16[64,1024]{1,0:T(8,128)(2,1)S(1)}, u32[]{:S(2)}, u32[]{:S(2)}) collective-permute-start(bf16[64,1024]{1,0:T(8,128)(2,1)} %param.7), channel_id=1, source_target_pairs={{0,1},{1,2},{2,3},{3,0},{4,5},{5,6},{6,7},{7,4},{8,9},{9,10},{10,1... | collective-permute-start | bytes 393224 | tf_op jit(solution)/shard_map/ppermute | solution.py:48
  15.4 6.8 %collective-permute-start.1 = (bf16[64,1024]{1,0:T(8,128)(2,1)S(1)}, bf16[64,1024]{1,0:T(8,128)(2,1)S(1)}, u32[]{:S(2)}, u32[]{:S(2)}) collective-permute-start(bf16[64,1024]{1,0:T(8,128)(2,1)S(1)} %collective-permute-done), channel_id=1, source_target_pairs={{0,1},{1,2},{2,3},{3,0},{4,5},{5,6},{6,7},{7,4},{8,9},{9,10},{10,1... | collective-permute-start | bytes 393224 | tf_op jit(solution)/shard_map/ppermute | solution.py:48
  22.2 6.8 %collective-permute-start.2 = (bf16[64,1024]{1,0:T(8,128)(2,1)S(1)}, bf16[64,1024]{1,0:T(8,128)(2,1)S(1)}, u32[]{:S(2)}, u32[]{:S(2)}) collective-permute-start(bf16[64,1024]{1,0:T(8,128)(2,1)S(1)} %collective-permute-done.1), channel_id=1, source_target_pairs={{0,1},{1,2},{2,3},{3,0},{4,5},{5,6},{6,7},{7,4},{8,9},{9,10},{10,1... | collective-permute-start | bytes 393224 | tf_op jit(solution)/shard_map/ppermute | solution.py:48
  87.0 4.2 %copy-start.2 = (s32[64,2]{0,1:T(2,128)S(1)}, s32[64,2]{0,1:T(2,128)}, u32[]{:S(2)}) copy-start(s32[64,2]{0,1:T(2,128)} %param.12) | copy-start | bytes 1540
  87.0 4.3 %copy-start.3 = (f32[64,2]{0,1:T(2,128)S(1)}, f32[64,2]{0,1:T(2,128)}, u32[]{:S(2)}) copy-start(f32[64,2]{0,1:T(2,128)} %param.13) | copy-start | bytes 1540
  87.1 29.4 %all-to-all-start.1 = ((f32[4,1,32,4096]{3,2,1,0:T(8,128)}), f32[4,1,32,4096]{3,2,1,0:T(8,128)S(1)}, u32[]{:S(2)}, u32[]{:S(2)}) async-start(f32[4,1,32,4096]{3,2,1,0:T(8,128)} %bitcast.29), calls=%async_computation.1 | async-start | bytes 4194304 | tf_op jit(solution)/shard_map/all_to_all | solution.py:67
  90.8 73.2 %reduce-scatter.2.cloned.1.call-start = ((), (), s32[]{:S(2)}) async-start(), calls=%async_computation.3 | async-start | bytes 1310720 | tf_op jit(solution)/shard_map/reduce_scatter | solution.py:81
Sparse Core Ops, SparseCore 0:
  139.4 24.5 reduce-scatter.1
